TPU v7x, 128 devices: a whole 4x4x4 slice. The times are simulated.
128 devices in a mesh: depth: 2 (over core), row: 16 (over z, x), col: 4 (over y).
Axes of the slice: x: 4, y: 4, z: 4, core: 2. Of those that a mesh axis runs over, the one named last changes fastest.
Arguments:
- right_side: bfloat16 [4, 16, 8, 128, 512], P(None, 'row', ('depth', 'col')), may hold values from -6 to 6
- inverse_diag: bfloat16 [4, 16, 8, 1, 128, 128], P(None, 'row', ('depth', 'col')), may hold values from -2 to 2.5, as said below
- coupling: bfloat16 [3, 16, 1024, 8, 2048], P(None, 'row', None, ('depth', 'col')), may hold values from -0.0625 to 0.0625
- pattern: int32 [3, 16, 8, 8, 16], P(None, 'row', None, ('depth', 'col')), may hold values 0 or 1
Outputs:
- forward_solution: bfloat16 [4, 16, 8, 128, 512], P(None, 'row', ('depth', 'col'))
- solution: bfloat16 [4, 16, 8, 128, 512], P(None, 'row', ('depth', 'col'))
Inputs may be any that keep to these rules, and one draw needn't show every extreme that they name: `inverse_diag`: each block is lower triangular with positive diagonal.
All inputs are finite; a program needn't handle non-finite values. No bound on the sum of `pattern` on one device may be relied on, other than what follows from the above.
Results may differ from a plain program's by a relative error of at most 0.025.
Values may be sent and summed in bfloat16 or wider, within the bound.
A program may use at most 128 MiB of HBM per device.

v0:
```python
import jax
import jax.numpy as jnp
from jax import lax
from jax.sharding import PartitionSpec as P


def apply_inverse(inverse, vector, transposed):
    blocks_in = vector.reshape(inverse.shape[0], inverse.shape[1], vector.shape[-1])
    einsum_form = "tji,tjn->tin" if transposed else "tij,tjn->tin"
    result = jnp.einsum(einsum_form, inverse, blocks_in, preferred_element_type=jnp.float32)
    return result.astype(jnp.bfloat16).reshape(vector.shape)


def lift_upward(masked, share_in):
    portion = lax.all_gather(share_in, "row", axis=0, tiled=True)
    span_rows = portion.shape[0] * portion.shape[2]
    return jnp.dot(
        masked, portion.reshape(span_rows, portion.shape[-1]), preferred_element_type=jnp.float32
    )


def carry_downward(masked, share_in):
    portion = lax.all_gather(share_in, ("depth", "col"), axis=1, tiled=True)
    span_rows = portion.shape[1] * portion.shape[2]
    return lax.dot_general(
        masked,
        portion.reshape(span_rows, portion.shape[-1]),
        (((0,), (0,)), ((), ())),
        preferred_element_type=jnp.float32,
    )


def forward_sum(partial_value, share_rows):
    blocks = partial_value.reshape(
        lax.axis_size(("depth", "col")), share_rows, partial_value.shape[-1]
    )
    summed = lax.psum(blocks.astype(jnp.bfloat16), ("depth", "col")).astype(jnp.float32)
    return lax.dynamic_index_in_dim(summed, lax.axis_index(("depth", "col")), 0, keepdims=False)


def backward_sum(partial_value, share_rows):
    blocks = partial_value.reshape(lax.axis_size("row"), share_rows, partial_value.shape[-1])
    summed = lax.psum(blocks.astype(jnp.bfloat16), "row").astype(jnp.float32)
    return lax.dynamic_index_in_dim(summed, lax.axis_index("row"), 0, keepdims=False)


def body(right_side, inverse_diag, coupling, pattern):
    levels = right_side.shape[0]
    share_rows = right_side.shape[3]
    rhs_cols = right_side.shape[4]
    block_width = inverse_diag.shape[-1]
    masked = []
    for pair_at in range(levels - 1):
        slab = coupling[pair_at, 0, :, 0, :]
        gate = pattern[pair_at, 0, :, 0, :].astype(jnp.bfloat16)
        shaped = (
            slab.reshape(gate.shape[0], block_width, gate.shape[1], block_width)
            * gate[:, None, :, None]
        )
        masked.append(shaped.reshape(slab.shape))
    panel_spans = [(0, rhs_cols)]
    fwd_levels = []
    for level_at in range(levels):
        pieces = []
        for panel_at, (col_first, col_last) in enumerate(panel_spans):
            source = right_side[level_at, 0, 0, :, col_first:col_last]
            if level_at == 0:
                residual = source
            else:
                partial_value = lift_upward(
                    masked[level_at - 1], fwd_levels[level_at - 1][panel_at][None, None]
                )
                residual = (
                    source.astype(jnp.float32) - forward_sum(partial_value, share_rows)
                ).astype(jnp.bfloat16)
            pieces.append(apply_inverse(inverse_diag[level_at, 0, 0], residual, False))
        fwd_levels.append(pieces)
    bwd_levels = [None] * levels
    for level_at in reversed(range(levels)):
        pieces = []
        panel_at = 0
        known_part = fwd_levels[level_at][panel_at]
        if level_at == levels - 1:
            residual = known_part
        else:
            partial_value = carry_downward(
                masked[level_at], bwd_levels[level_at + 1][panel_at][None, None]
            )
            residual = (
                known_part.astype(jnp.float32) - backward_sum(partial_value, share_rows)
            ).astype(jnp.bfloat16)
        pieces.append(apply_inverse(inverse_diag[level_at, 0, 0], residual, True))
        bwd_levels[level_at] = pieces
    forward_rows = []
    backward_rows = []
    for level_at in range(levels):
        forward_rows.append(jnp.concatenate(fwd_levels[level_at], axis=1))
        backward_rows.append(jnp.concatenate(bwd_levels[level_at], axis=1))
    forward_solution = jnp.stack(forward_rows).reshape(levels, 1, 1, share_rows, rhs_cols)
    solution = jnp.stack(backward_rows).reshape(levels, 1, 1, share_rows, rhs_cols)
    return (forward_solution, solution)


def solution(mesh):
    placed = (
        P(None, "row", ("depth", "col"), None, None),
        P(None, "row", ("depth", "col"), None, None, None),
        P(None, "row", None, ("depth", "col"), None),
        P(None, "row", None, ("depth", "col"), None),
    )
    return jax.shard_map(
        body,
        mesh=mesh,
        in_specs=placed,
        out_specs=(
            P(None, "row", ("depth", "col"), None, None),
            P(None, "row", ("depth", "col"), None, None),
        ),
        check_vma=False,
    )
```

profile of v0, /device:TPU:0, one launch (start us, length us, event | category | flops | bytes accessed | tf_op | source)
XLA Modules:
  0.0 735.9 jit_solution(18099699853977080136)
XLA Ops:
  7.2 1.8 convolution_convert_fusion.10
  9.0 0.7 convert.11
  9.8 2.6 mul.62
  12.3 7.3 mul.63
  19.6 2.6 mul.71
  22.2 7.3 mul.72
  29.6 2.6 mul.67
  32.2 7.4 mul.68
  39.5 13.6 %slice_multiply_fusion.2 = (bf16[1,1,1024,1,2048]{4,2,3,1,0:T(8,128)(2,1)}, bf16[1,1,1024,1,2048]{4,2,3,1,0:T(8,128)(2,1)}, bf16[1,1,1024,1,2048]{4,2,3,1,0:T(8,128)(2,1)}) fusion(bf16[1,1,1024,1,2048]{4,2,3,1,0:T(8,128)(2,1)} %mul.63, bf16[3,1,1024,1,2048]{4,2,3,1,0:T(8,128)(2,1)} %param.6, bf16[1,1,1024,1,2048]{4,2,3,1,0:T(8,128)(2,1)} %mul.72, ...), kind=kLoop, calls=%fused_computation.8 | loop fusion | flops 6291456 | bytes 37748736 | tf_op jit(solution)/shard_map/mul | solution.py:57
  53.1 5.1 all-gather.13.cloned.1.call-done
  58.2 6.2 fusion.9
  64.5 62.1 %all-reduce.7.cloned.1.call-done = bf16[8,128,512]{2,1,0:T(8,128)(2,1)} async-done(((bf16[8,128,512]{2,1,0:T(8,128)(2,1)}), bf16[8,128,512]{2,1,0:T(8,128)(2,1)}) %all-reduce.7.cloned.1.call-update) | async-done | bytes 1048592 | tf_op jit(solution)/shard_map/psum | solution.py:37
  126.6 1.7 convolution_convert_fusion.5
  128.4 0.0 all-reduce.9.cloned.1.call-start
  128.5 45.3 %all-gather.15.cloned.1.call-done = bf16[2048,512]{1,0:T(8,128)(2,1)} async-done(((bf16[128,512]{1,0:T(8,128)(2,1)}), bf16[2048,512]{1,0:T(8,128)(2,1)}) %all-gather.15.cloned.1.call-update) | async-done | bytes 2097168 | tf_op jit(solution)/shard_map/all_gather | solution.py:15
  173.7 6.2 fusion.12
  180.0 0.0 all-gather.17.cloned.1.call-start
  180.0 62.1 %all-reduce.9.cloned.1.call-done = bf16[8,128,512]{2,1,0:T(8,128)(2,1)} async-done(((bf16[8,128,512]{2,1,0:T(8,128)(2,1)}), bf16[8,128,512]{2,1,0:T(8,128)(2,1)}) %all-reduce.9.cloned.1.call-update) | async-done | bytes 1048592 | tf_op jit(solution)/shard_map/psum | solution.py:37
  242.1 1.7 convolution_convert_fusion.4
  243.9 0.0 all-reduce.11.cloned.1.call-start
  243.9 44.5 %all-gather.17.cloned.1.call-done = bf16[2048,512]{1,0:T(8,128)(2,1)} async-done(((bf16[128,512]{1,0:T(8,128)(2,1)}), bf16[2048,512]{1,0:T(8,128)(2,1)}) %all-gather.17.cloned.1.call-update) | async-done | bytes 2097168 | tf_op jit(solution)/shard_map/all_gather | solution.py:15
  288.5 6.2 fusion.15
  294.7 0.0 all-gather.19.cloned.1.call-start
  294.7 62.1 %all-reduce.11.cloned.1.call-done = bf16[8,128,512]{2,1,0:T(8,128)(2,1)} async-done(((bf16[8,128,512]{2,1,0:T(8,128)(2,1)}), bf16[8,128,512]{2,1,0:T(8,128)(2,1)}) %all-reduce.11.cloned.1.call-update) | async-done | bytes 1048592 | tf_op jit(solution)/shard_map/psum | solution.py:37
  356.8 1.1 convolution_convert_fusion.3
  357.9 0.9 convolution_convert_fusion.9
  358.8 0.2 all-reduce.13.cloned.1.call-start
  359.0 15.1 %fusion.2 = (bf16[2048,1024]{0,1:T(8,128)(2,1)}, bf16[2048,1024]{0,1:T(8,128)(2,1)}, bf16[2048,1024]{0,1:T(8,128)(2,1)}) fusion(bf16[128,8,16,128]{3,2,1,0:T(8,128)(2,1)} %bitcast.180, bf16[3,1,1024,1,2048]{4,2,3,1,0:T(8,128)(2,1)} %param.6, bf16[128,8,16,128]{3,2,1,0:T(8,128)(2,1)} %bitcast.182, bf16[128,8,16,128]{3,2,1,0:T(8,128)(2,1)} %bitcast.181), kind=kLoop, calls=%fused_computation.5 | loop fusion | flops 6291456 | bytes 37748736 | tf_op jit(solution)/shard_map/dot_general | solution.py:25
  374.1 6.4 copy.26
  380.5 1.1 all-gather.19.cloned.1.call-done
  381.6 6.3 convolution_convert_fusion.2
  387.9 92.3 %all-reduce.13.cloned.1.call-done = bf16[16,128,512]{2,1,0:T(8,128)(2,1)} async-done(((bf16[16,128,512]{2,1,0:T(8,128)(2,1)}), bf16[16,128,512]{2,1,0:T(8,128)(2,1)}) %all-reduce.13.cloned.1.call-update) | async-done | bytes 2097168 | tf_op jit(solution)/shard_map/psum | solution.py:43
  480.2 1.8 convolution_convert_fusion.8
  482.0 0.0 all-reduce.15.cloned.1.call-start
  482.1 6.4 copy.25
  488.5 16.4 %all-gather.21.cloned.1.call-done = bf16[1024,512]{0,1:T(8,128)(2,1)} async-done(((bf16[128,512]{0,1:T(8,128)(2,1)}), bf16[1024,512]{0,1:T(8,128)(2,1)}) %all-gather.21.cloned.1.call-update) | async-done | bytes 1048592 | tf_op jit(solution)/shard_map/all_gather | solution.py:23
  504.9 6.3 convolution_convert_fusion.1
  511.2 92.3 %all-reduce.15.cloned.1.call-done = bf16[16,128,512]{2,1,0:T(8,128)(2,1)} async-done(((bf16[16,128,512]{2,1,0:T(8,128)(2,1)}), bf16[16,128,512]{2,1,0:T(8,128)(2,1)}) %all-reduce.15.cloned.1.call-update) | async-done | bytes 2097168 | tf_op jit(solution)/shard_map/psum | solution.py:43
  603.5 1.8 convolution_convert_fusion.7
  605.3 0.0 all-reduce.17.cloned.1.call-start
  605.3 6.4 copy.24
  611.7 16.4 %all-gather.23.cloned.1.call-done = bf16[1024,512]{0,1:T(8,128)(2,1)} async-done(((bf16[128,512]{0,1:T(8,128)(2,1)}), bf16[1024,512]{0,1:T(8,128)(2,1)}) %all-gather.23.cloned.1.call-update) | async-done | bytes 1048592 | tf_op jit(solution)/shard_map/all_gather | solution.py:23
  628.2 6.3 convolution_convert_fusion
  634.5 0.9 maximum_bitcast_fusion
  635.3 91.5 %all-reduce.17.cloned.1.call-done = bf16[16,128,512]{2,1,0:T(8,128)(2,1)} async-done(((bf16[16,128,512]{2,1,0:T(8,128)(2,1)}), bf16[16,128,512]{2,1,0:T(8,128)(2,1)}) %all-reduce.17.cloned.1.call-update) | async-done | bytes 2097168 | tf_op jit(solution)/shard_map/psum | solution.py:43
  726.8 1.1 fusion.18
  728.0 0.1 maximum_bitcast_fusion.1
  728.1 1.0 copy.17
  (34 shorter events, 0.4 us)
Async XLA Ops:
  7.2 51.1 %all-gather.13.cloned.1.call-start = ((), (), s32[]{:S(2)}) async-start(), calls=%async_computation.6 | async-start | bytes 2228224 | tf_op jit(solution)/shard_map/all_gather | solution.py:15
  9.0 117.6 %all-reduce.7.cloned.1.call-start = ((), (), s32[]{:S(2)}) async-start(), calls=%async_computation | async-start | bytes 2097152 | tf_op jit(solution)/shard_map/psum | solution.py:37
  58.2 68.4 %copy-start.6 = (bf16[4,1,1,128,512]{4,3,2,1,0:T(8,128)(2,1)S(1)}, bf16[4,1,1,128,512]{4,3,2,1,0:T(8,128)(2,1)}, u32[]{:S(2)}) copy-start(bf16[4,1,1,128,512]{4,3,2,1,0:T(8,128)(2,1)} %param.4) | copy-start | bytes 1572868
  58.2 68.4 %copy-start.7 = (bf16[4,1,1,1,128,128]{5,4,3,2,1,0:T(8,128)(2,1)S(1)}, bf16[4,1,1,1,128,128]{5,4,3,2,1,0:T(8,128)(2,1)}, u32[]{:S(2)}) copy-start(bf16[4,1,1,1,128,128]{5,4,3,2,1,0:T(8,128)(2,1)} %param.5) | copy-start | bytes 393220
  64.5 109.2 %all-gather.15.cloned.1.call-start = ((), (), s32[]{:S(2)}) async-start(), calls=%async_computation.7 | async-start | bytes 2228224 | tf_op jit(solution)/shard_map/all_gather | solution.py:15
  128.4 113.7 %all-reduce.9.cloned.1.call-start = ((), (), s32[]{:S(2)}) async-start(), calls=%async_computation.1 | async-start | bytes 2097152 | tf_op jit(solution)/shard_map/psum | solution.py:37
  180.0 108.5 %all-gather.17.cloned.1.call-start = ((), (), s32[]{:S(2)}) async-start(), calls=%async_computation.8 | async-start | bytes 2228224 | tf_op jit(solution)/shard_map/all_gather | solution.py:15
  243.9 113.0 %all-reduce.11.cloned.1.call-start = ((), (), s32[]{:S(2)}) async-start(), calls=%async_computation.2 | async-start | bytes 2097152 | tf_op jit(solution)/shard_map/psum | solution.py:37
  294.7 86.9 %all-gather.19.cloned.1.call-start = ((), (), s32[]{:S(2)}) async-start(), calls=%async_computation.9 | async-start | bytes 1179648 | tf_op jit(solution)/shard_map/all_gather | solution.py:23
  358.8 121.4 %all-reduce.13.cloned.1.call-start = ((), (), s32[]{:S(2)}) async-start(), calls=%async_computation.3 | async-start | bytes 4194304 | tf_op jit(solution)/shard_map/psum | solution.py:43
  381.6 98.7 %copy-start.2 = (bf16[512,128]{0,1:T(8,128)(2,1)S(1)}, bf16[512,128]{0,1:T(8,128)(2,1)}, u32[]{:S(2)}) copy-start(bf16[512,128]{0,1:T(8,128)(2,1)} %convolution_convert_fusion.4) | copy-start | bytes 393220
  387.9 117.0 %all-gather.21.cloned.1.call-start = ((), (), s32[]{:S(2)}) async-start(), calls=%async_computation.10 | async-start | bytes 1179648 | tf_op jit(solution)/shard_map/all_gather | solution.py:23
  482.0 121.4 %all-reduce.15.cloned.1.call-start = ((), (), s32[]{:S(2)}) async-start(), calls=%async_computation.4 | async-start | bytes 4194304 | tf_op jit(solution)/shard_map/psum | solution.py:43
  504.9 98.6 %copy-start.1 = (bf16[512,128]{0,1:T(8,128)(2,1)S(1)}, bf16[512,128]{0,1:T(8,128)(2,1)}, u32[]{:S(2)}) copy-start(bf16[512,128]{0,1:T(8,128)(2,1)} %convolution_convert_fusion.5) | copy-start | bytes 393220
  511.2 117.0 %all-gather.23.cloned.1.call-start = ((), (), s32[]{:S(2)}) async-start(), calls=%async_computation.11 | async-start | bytes 1179648 | tf_op jit(solution)/shard_map/all_gather | solution.py:23
  605.3 121.5 %all-reduce.17.cloned.1.call-start = ((), (), s32[]{:S(2)}) async-start(), calls=%async_computation.5 | async-start | bytes 4194304 | tf_op jit(solution)/shard_map/psum | solution.py:43
  628.1 6.3 copy-start
  628.1 99.8 %copy-start.3 = (bf16[512,128]{1,0:T(8,128)(2,1)S(1)}, bf16[512,128]{1,0:T(8,128)(2,1)}, u32[]{:S(2)}) copy-start(bf16[512,128]{1,0:T(8,128)(2,1)} %convolution_convert_fusion.9) | copy-start | bytes 393220
  628.1 99.8 %copy-start.4 = (bf16[512,128]{1,0:T(8,128)(2,1)S(1)}, bf16[512,128]{1,0:T(8,128)(2,1)}, u32[]{:S(2)}) copy-start(bf16[512,128]{1,0:T(8,128)(2,1)} %convolution_convert_fusion.8) | copy-start | bytes 393220
  628.2 99.8 %copy-start.5 = (bf16[512,128]{1,0:T(8,128)(2,1)S(1)}, bf16[512,128]{1,0:T(8,128)(2,1)}, u32[]{:S(2)}) copy-start(bf16[512,128]{1,0:T(8,128)(2,1)} %convolution_convert_fusion.7) | copy-start | bytes 393220
Sparse Core Ops, SparseCore 0:
  10.7 47.4 all-gather.12
  64.6 61.9 all-reduce.6
  129.4 44.3 all-gather.14
  180.1 61.9 all-reduce.8
  244.1 44.3 all-gather.16
  294.8 61.9 all-reduce.10
  358.9 22.6 all-gather.18
  388.0 92.1 all-reduce.12
  482.2 22.6 all-gather.20
  511.3 92.1 all-reduce.14
  605.4 22.6 all-gather.22
  634.6 92.1 all-reduce.16
where the time goes:
time: 737 us; the launch traced here: 736 us
  waiting for transfers between devices  591 us (80%)
  local copies, waits for them, and re-layouts  50 us (7%)
  matrix products  49.3 us (7%)
  other arithmetic  30.3 us (4%)
  between operations  14.3 us (2%)
    psum x3, waiting for transfers between devices, backward_sum(): summed = lax.psum(blocks.astype(jnp.bfloat16), 'row').astype(jnp.float32)  276 us
    psum x3, waiting for transfers between devices, forward_sum(): lax.psum(blocks.astype(jnp.bfloat16), ('depth', 'col')).astype(jnp.float32)  186 us
    all_gather x3, waiting for transfers between devices, lift_upward(): portion = lax.all_gather(share_in, 'row', axis=0, tiled=True)  94.9 us
    all_gather x3, waiting for transfers between devices, carry_downward(): portion = lax.all_gather(share_in, ('depth', 'col'), axis=1, tiled=True)  33.9 us
    mul x6, local copies, waits for them, and re-layouts, body(): slab.reshape(gate.shape[0], block_width, gate.shape[1], block_width)  29.7 us
    dot_general x3, local copies, waits for them, and re-layouts, carry_downward(): lax.dot_general(masked, portion.reshape(span_rows, portion.shape[-1]), ((...  19.2 us
    dot_general x3, matrix products, carry_downward(): lax.dot_general(masked, portion.reshape(span_rows, portion.shape[-1]), ((...  18.8 us
    dot_general x3, matrix products, lift_upward(): jnp.dot(masked, portion.reshape(span_rows, portion.shape[-1]), preferred_...  18.6 us
  transfers between devices with their start and end apart: 12, of which 12 were waited for; matrix products, arithmetic and copies ran while one was open for 11% of the time, Pallas kernels for 0%

commit v1 on v0

--- a/solution.py
+++ b/solution.py
@@ -12,7 +12,9 @@
 
 
 def lift_upward(masked, share_in):
-    portion = lax.all_gather(share_in, "row", axis=0, tiled=True)
+    portion = jnp.concatenate(
+        lax.all_to_all(jnp.stack([share_in] * lax.axis_size("row")), "row", 0, 0), axis=0
+    )
     span_rows = portion.shape[0] * portion.shape[2]
     return jnp.dot(
         masked, portion.reshape(span_rows, portion.shape[-1]), preferred_element_type=jnp.float32

time: 737 us -> 710 us (0.963)
  waiting for transfers between devices: 591 us -> 497 us
  blocking collectives: 0 us -> 66.6 us
  matrix products: 49.3 us -> 41.2 us
  starting transfers between devices: 0.68 us -> 8.55 us
    all_gather x3 -> x0, waiting for transfers between devices: 94.9 us -> none  [lift_upward(): portion = lax.all_gather(share_in, 'row', axis=0, tiled=True)]
    all_to_all x0 -> x2, blocking collectives: none -> 66.6 us  [lift_upward(): lax.all_to_all(jnp.stack([share_in] * lax.axis_size('row')), 'row', 0, 0)]
    all_to_all x0 -> x1, starting transfers between devices: none -> 7.99 us  [lift_upward(): lax.all_to_all(jnp.stack([share_in] * lax.axis_size('row')), 'row', 0, 0)]
  transfers between devices with their start and end apart: 12 -> 10, of which waited for: 12 -> 9; matrix products, arithmetic and copies ran while one was open for 11% -> 11% of each run, Pallas kernels for 0% -> 0%
where the time goes in v1:
time: 710 us; the launch traced here: 709 us
  waiting for transfers between devices  497 us (70%)
  blocking collectives  66.6 us (9%)
  local copies, waits for them, and re-layouts  51.9 us (7%)
  matrix products  41.2 us (6%)
  other arithmetic  29.3 us (4%)
  between operations  14 us (2%)
  starting transfers between devices  8.55 us (1%)
    psum x3, waiting for transfers between devices, backward_sum(): summed = lax.psum(blocks.astype(jnp.bfloat16), 'row').astype(jnp.float32)  276 us
    psum x3, waiting for transfers between devices, forward_sum(): lax.psum(blocks.astype(jnp.bfloat16), ('depth', 'col')).astype(jnp.float32)  187 us
    all_to_all x2, blocking collectives, lift_upward(): lax.all_to_all(jnp.stack([share_in] * lax.axis_size('row')), 'row', 0, 0)  66.6 us
    all_gather x3, waiting for transfers between devices, carry_downward(): portion = lax.all_gather(share_in, ('depth', 'col'), axis=1, tiled=True)  33.9 us
    mul x6, local copies, waits for them, and re-layouts, body(): slab.reshape(gate.shape[0], block_width, gate.shape[1], block_width)  29.6 us
    dot_general x3, local copies, waits for them, and re-layouts, carry_downward(): lax.dot_general(masked, portion.reshape(span_rows, portion.shape[-1]), ((...  19.2 us
    dot_general x3, matrix products, carry_downward(): lax.dot_general(masked, portion.reshape(span_rows, portion.shape[-1]), ((...  18.7 us
    dot_general x1, other arithmetic, carry_downward(): lax.dot_general(masked, portion.reshape(span_rows, portion.shape[-1]), ((...  15.1 us
  transfers between devices with their start and end apart: 10, of which 9 were waited for; matrix products, arithmetic and copies ran while one was open for 11% of the time, Pallas kernels for 0%

profile of v1, /device:TPU:0, one launch (start us, length us, event | category | flops | bytes accessed | tf_op | source)
XLA Modules:
  0.0 708.6 jit_solution(9963009346857900268)
XLA Ops:
  7.2 1.1 convolution_convert_fusion.13
  8.3 1.6 stack.15
  9.9 8.0 %all-to-all-start = ((bf16[16,1,1,128,512]{4,3,2,1,0:T(8,128)(2,1)}), bf16[16,1,1,128,512]{4,3,2,1,0:T(8,128)(2,1)S(1)}, u32[]{:S(2)}, u32[]{:S(2)}) async-start(bf16[16,1,1,128,512]{4,3,2,1,0:T(8,128)(2,1)} %stack.15), calls=%async_computation | async-start | bytes 4194304 | tf_op jit(solution)/shard_map/all_to_all | solution.py:16
  17.9 2.5 mul.62
  20.5 7.3 %mul.63 = bf16[1,1,1024,1,2048]{4,2,3,1,0:T(8,128)(2,1)} reshape(bf16[8,128,16,128]{3,2,1,0:T(8,128)(2,1)} %mul.62) | data formatting | bytes 8388608 | tf_op jit(solution)/shard_map/mul | solution.py:59
  27.8 2.6 mul.71
  30.4 7.3 %mul.72 = bf16[1,1,1024,1,2048]{4,2,3,1,0:T(8,128)(2,1)} reshape(bf16[8,128,16,128]{3,2,1,0:T(8,128)(2,1)} %mul.71) | data formatting | bytes 8388608 | tf_op jit(solution)/shard_map/mul | solution.py:59
  37.7 2.6 mul.67
  40.3 7.3 %mul.68 = bf16[1,1,1024,1,2048]{4,2,3,1,0:T(8,128)(2,1)} reshape(bf16[8,128,16,128]{3,2,1,0:T(8,128)(2,1)} %mul.67) | data formatting | bytes 8388608 | tf_op jit(solution)/shard_map/mul | solution.py:59
  47.6 13.3 %slice_multiply_fusion.2 = (bf16[1,1,1024,1,2048]{4,2,3,1,0:T(8,128)(2,1)}, bf16[1,1,1024,1,2048]{4,2,3,1,0:T(8,128)(2,1)}, bf16[1,1,1024,1,2048]{4,2,3,1,0:T(8,128)(2,1)}) fusion(bf16[1,1,1024,1,2048]{4,2,3,1,0:T(8,128)(2,1)} %mul.63, bf16[3,1,1024,1,2048]{4,2,3,1,0:T(8,128)(2,1)} %param.6, bf16[1,1,1024,1,2048]{4,2,3,1,0:T(8,128)(2,1)} %mul.72, ...), kind=kLoop, calls=%fused_computation.8 | loop fusion | flops 6291456 | bytes 37748736 | tf_op jit(solution)/shard_map/mul | solution.py:59
  60.9 5.6 convolution_convert_fusion.5
  66.6 0.0 all-reduce.9.cloned.1.call-start
  66.6 64.5 %all-reduce.7.cloned.1.call-done = bf16[8,128,512]{2,1,0:T(8,128)(2,1)} async-done(((bf16[8,128,512]{2,1,0:T(8,128)(2,1)}), bf16[8,128,512]{2,1,0:T(8,128)(2,1)}) %all-reduce.7.cloned.1.call-update) | async-done | bytes 1048592 | tf_op jit(solution)/shard_map/psum | solution.py:39
  131.1 1.2 convolution_convert_fusion.8
  132.4 0.2 stack.16
  132.6 33.3 %all_to_all.15 = bf16[16,1,1,128,512]{4,3,2,1,0:T(8,128)(2,1)S(1)} all-to-all(bf16[16,1,1,128,512]{4,3,2,1,0:T(8,128)(2,1)S(1)} %stack.16), channel_id=1, replica_groups=mesh['depth'=2,'row'=16,'col'=4] {'row'}, dimensions={0} | all-to-all | bytes 4194304 | tf_op jit(solution)/shard_map/all_to_all | solution.py:16
  165.9 3.3 convolution_convert_fusion.4
  169.3 61.3 %all-reduce.9.cloned.1.call-done = bf16[8,128,512]{2,1,0:T(8,128)(2,1)} async-done(((bf16[8,128,512]{2,1,0:T(8,128)(2,1)}), bf16[8,128,512]{2,1,0:T(8,128)(2,1)}) %all-reduce.9.cloned.1.call-update) | async-done | bytes 1048592 | tf_op jit(solution)/shard_map/psum | solution.py:39
  230.6 1.2 convolution_convert_fusion.7
  231.8 0.2 stack.17
  232.0 33.3 %all_to_all.16 = bf16[16,1,1,128,512]{4,3,2,1,0:T(8,128)(2,1)S(1)} all-to-all(bf16[16,1,1,128,512]{4,3,2,1,0:T(8,128)(2,1)S(1)} %stack.17), channel_id=1, replica_groups=mesh['depth'=2,'row'=16,'col'=4] {'row'}, dimensions={0} | all-to-all | bytes 4194304 | tf_op jit(solution)/shard_map/all_to_all | solution.py:16
  265.3 3.3 convolution_convert_fusion.3
  268.7 0.0 all-gather.7.cloned.1.call-start
  268.7 61.2 %all-reduce.11.cloned.1.call-done = bf16[8,128,512]{2,1,0:T(8,128)(2,1)} async-done(((bf16[8,128,512]{2,1,0:T(8,128)(2,1)}), bf16[8,128,512]{2,1,0:T(8,128)(2,1)}) %all-reduce.11.cloned.1.call-update) | async-done | bytes 1048592 | tf_op jit(solution)/shard_map/psum | solution.py:39
  329.9 1.1 convolution_convert_fusion.6
  331.0 0.9 convolution_convert_fusion.12
  331.9 0.2 all-reduce.13.cloned.1.call-start
  332.1 15.1 %fusion.2 = (bf16[2048,1024]{0,1:T(8,128)(2,1)}, bf16[2048,1024]{0,1:T(8,128)(2,1)}, bf16[2048,1024]{0,1:T(8,128)(2,1)}) fusion(bf16[128,8,16,128]{3,2,1,0:T(8,128)(2,1)} %bitcast.177, bf16[3,1,1024,1,2048]{4,2,3,1,0:T(8,128)(2,1)} %param.6, bf16[128,8,16,128]{3,2,1,0:T(8,128)(2,1)} %bitcast.179, bf16[128,8,16,128]{3,2,1,0:T(8,128)(2,1)} %bitcast.178), kind=kLoop, calls=%fused_computation.5 | loop fusion | flops 6291456 | bytes 37748736 | tf_op jit(solution)/shard_map/dot_general | solution.py:27
  347.2 6.4 copy.38
  353.6 1.1 all-gather.7.cloned.1.call-done
  354.7 6.2 convolution_convert_fusion.2
  360.9 0.0 all-gather.9.cloned.1.call-start
  361.0 92.3 %all-reduce.13.cloned.1.call-done = bf16[16,128,512]{2,1,0:T(8,128)(2,1)} async-done(((bf16[16,128,512]{2,1,0:T(8,128)(2,1)}), bf16[16,128,512]{2,1,0:T(8,128)(2,1)}) %all-reduce.13.cloned.1.call-update) | async-done | bytes 2097168 | tf_op jit(solution)/shard_map/psum | solution.py:45
  453.3 1.8 convolution_convert_fusion.11
  455.1 0.0 all-reduce.15.cloned.1.call-start
  455.1 6.4 copy.37
  461.5 16.4 %all-gather.9.cloned.1.call-done = bf16[1024,512]{0,1:T(8,128)(2,1)} async-done(((bf16[128,512]{0,1:T(8,128)(2,1)}), bf16[1024,512]{0,1:T(8,128)(2,1)}) %all-gather.9.cloned.1.call-update) | async-done | bytes 1048592 | tf_op jit(solution)/shard_map/all_gather | solution.py:25
  477.9 6.2 convolution_convert_fusion.1
  484.2 92.3 %all-reduce.15.cloned.1.call-done = bf16[16,128,512]{2,1,0:T(8,128)(2,1)} async-done(((bf16[16,128,512]{2,1,0:T(8,128)(2,1)}), bf16[16,128,512]{2,1,0:T(8,128)(2,1)}) %all-reduce.15.cloned.1.call-update) | async-done | bytes 2097168 | tf_op jit(solution)/shard_map/psum | solution.py:45
  576.5 1.8 convolution_convert_fusion.10
  578.3 6.4 copy.36
  584.8 16.4 %all-gather.11.cloned.1.call-done = bf16[1024,512]{0,1:T(8,128)(2,1)} async-done(((bf16[128,512]{0,1:T(8,128)(2,1)}), bf16[1024,512]{0,1:T(8,128)(2,1)}) %all-gather.11.cloned.1.call-update) | async-done | bytes 1048592 | tf_op jit(solution)/shard_map/all_gather | solution.py:25
  601.2 6.3 convolution_convert_fusion
  607.4 0.9 maximum_bitcast_fusion
  608.3 91.5 %all-reduce.17.cloned.1.call-done = bf16[16,128,512]{2,1,0:T(8,128)(2,1)} async-done(((bf16[16,128,512]{2,1,0:T(8,128)(2,1)}), bf16[16,128,512]{2,1,0:T(8,128)(2,1)}) %all-reduce.17.cloned.1.call-update) | async-done | bytes 2097168 | tf_op jit(solution)/shard_map/psum | solution.py:45
  699.8 1.1 fusion.3
  701.0 0.1 maximum_bitcast_fusion.1
  701.1 1.0 copy.29
  (32 shorter events, 0.4 us)
Async XLA Ops:
  7.2 10.8 %copy-start.7 = (s32[3,1,8,1,16]{4,3,2,1,0:T(1,128)S(1)}, s32[3,1,8,1,16]{4,3,2,1,0:T(1,128)}, u32[]{:S(2)}) copy-start(s32[3,1,8,1,16]{4,3,2,1,0:T(1,128)} %param.7) | copy-start | bytes 4612
  9.9 51.0 %all-to-all-start = ((bf16[16,1,1,128,512]{4,3,2,1,0:T(8,128)(2,1)}), bf16[16,1,1,128,512]{4,3,2,1,0:T(8,128)(2,1)S(1)}, u32[]{:S(2)}, u32[]{:S(2)}) async-start(bf16[16,1,1,128,512]{4,3,2,1,0:T(8,128)(2,1)} %stack.15), calls=%async_computation | async-start | bytes 4194304 | tf_op jit(solution)/shard_map/all_to_all | solution.py:16
  17.9 113.2 %all-reduce.7.cloned.1.call-start = ((), (), s32[]{:S(2)}) async-start(), calls=%async_computation.3 | async-start | bytes 2097152 | tf_op jit(solution)/shard_map/psum | solution.py:39
  60.9 70.2 %copy-start.5 = (bf16[4,1,1,128,512]{4,3,2,1,0:T(8,128)(2,1)S(1)}, bf16[4,1,1,128,512]{4,3,2,1,0:T(8,128)(2,1)}, u32[]{:S(2)}) copy-start(bf16[4,1,1,128,512]{4,3,2,1,0:T(8,128)(2,1)} %param.4) | copy-start | bytes 1572868
  60.9 70.2 %copy-start.6 = (bf16[4,1,1,1,128,128]{5,4,3,2,1,0:T(8,128)(2,1)S(1)}, bf16[4,1,1,1,128,128]{5,4,3,2,1,0:T(8,128)(2,1)}, u32[]{:S(2)}) copy-start(bf16[4,1,1,1,128,128]{5,4,3,2,1,0:T(8,128)(2,1)} %param.5) | copy-start | bytes 393220
  66.6 164.0 %all-reduce.9.cloned.1.call-start = ((), (), s32[]{:S(2)}) async-start(), calls=%async_computation.4 | async-start | bytes 2097152 | tf_op jit(solution)/shard_map/psum | solution.py:39
  131.1 34.8 %copy-start.1 = (bf16[1,1,1024,1,2048]{4,2,3,1,0:T(8,128)(2,1)S(1)}, bf16[1,1,1024,1,2048]{4,2,3,1,0:T(8,128)(2,1)}, u32[]{:S(2)}) copy-start(bf16[1,1,1024,1,2048]{4,2,3,1,0:T(8,128)(2,1)} %get-tuple-element.11) | copy-start | bytes 12582916
  169.2 160.7 %all-reduce.11.cloned.1.call-start = ((), (), s32[]{:S(2)}) async-start(), calls=%async_computation.5 | async-start | bytes 2097152 | tf_op jit(solution)/shard_map/psum | solution.py:39
  230.6 34.8 %copy-start = (bf16[1,1,1024,1,2048]{4,2,3,1,0:T(8,128)(2,1)S(1)}, bf16[1,1,1024,1,2048]{4,2,3,1,0:T(8,128)(2,1)}, u32[]{:S(2)}) copy-start(bf16[1,1,1024,1,2048]{4,2,3,1,0:T(8,128)(2,1)} %get-tuple-element.10) | copy-start | bytes 12582916
  268.7 86.0 %all-gather.7.cloned.1.call-start = ((), (), s32[]{:S(2)}) async-start(), calls=%async_computation.9 | async-start | bytes 1179648 | tf_op jit(solution)/shard_map/all_gather | solution.py:25
  331.9 121.4 %all-reduce.13.cloned.1.call-start = ((), (), s32[]{:S(2)}) async-start(), calls=%async_computation.6 | async-start | bytes 4194304 | tf_op jit(solution)/shard_map/psum | solution.py:45
  360.9 117.0 %all-gather.9.cloned.1.call-start = ((), (), s32[]{:S(2)}) async-start(), calls=%async_computation.10 | async-start | bytes 1179648 | tf_op jit(solution)/shard_map/all_gather | solution.py:25
  455.1 121.5 %all-reduce.15.cloned.1.call-start = ((), (), s32[]{:S(2)}) async-start(), calls=%async_computation.7 | async-start | bytes 4194304 | tf_op jit(solution)/shard_map/psum | solution.py:45
  484.2 117.0 %all-gather.11.cloned.1.call-start = ((), (), s32[]{:S(2)}) async-start(), calls=%async_computation.11 | async-start | bytes 1179648 | tf_op jit(solution)/shard_map/all_gather | solution.py:25
  578.3 121.5 %all-reduce.17.cloned.1.call-start = ((), (), s32[]{:S(2)}) async-start(), calls=%async_computation.8 | async-start | bytes 4194304 | tf_op jit(solution)/shard_map/psum | solution.py:45
  601.2 99.8 %copy-start.2 = (bf16[512,128]{1,0:T(8,128)(2,1)S(1)}, bf16[512,128]{1,0:T(8,128)(2,1)}, u32[]{:S(2)}) copy-start(bf16[512,128]{1,0:T(8,128)(2,1)} %convolution_convert_fusion.12) | copy-start | bytes 393220
  601.2 99.8 %copy-start.3 = (bf16[512,128]{1,0:T(8,128)(2,1)S(1)}, bf16[512,128]{1,0:T(8,128)(2,1)}, u32[]{:S(2)}) copy-start(bf16[512,128]{1,0:T(8,128)(2,1)} %convolution_convert_fusion.11) | copy-start | bytes 393220
  601.2 99.8 %copy-start.4 = (bf16[512,128]{1,0:T(8,128)(2,1)S(1)}, bf16[512,128]{1,0:T(8,128)(2,1)}, u32[]{:S(2)}) copy-start(bf16[512,128]{1,0:T(8,128)(2,1)} %convolution_convert_fusion.10) | copy-start | bytes 393220
Sparse Core Ops, SparseCore 0:
  66.7 64.3 all-reduce.6
  169.3 61.1 all-reduce.8
  268.8 61.0 all-reduce.10
  332.0 22.6 all-gather.6
  361.0 92.1 all-reduce.12
  455.2 22.6 all-gather.8
  484.3 92.1 all-reduce.14
  578.4 22.6 all-gather.10
  607.6 92.2 all-reduce.16
